TPU v7x, 32 devices: a whole 2x2x4 slice. The times are simulated.
32 devices in a mesh: seq: 8 (over z, y), tp: 4 (over x, core).
Axes of the slice: x: 2, y: 2, z: 4, core: 2. Of those that a mesh axis runs over, the one named last changes fastest.
Arguments:
- mixer_input: bfloat16 [1024, 8192], P('seq', 'tp'), may hold values from -6 to 6
- gate_input: bfloat16 [1024, 8192], P('seq', 'tp'), may hold values from -6 to 6
- input_matrix: bfloat16 [1024, 1024], P('seq', 'tp'), may hold values from -6 to 6
- output_matrix: bfloat16 [1024, 1024], P('seq', 'tp'), may hold values from -6 to 6
- step_raw: float32 [1024, 128], P('seq', 'tp'), may hold values from -3 to 3
- step_bias: float32 [128], P('tp'), may hold values from -1 to 0.5
- decay_rate: float32 [128], P('tp'), may hold values from 0.0001 to 0.05
- skip_weight: float32 [128], P('tp'), may hold values from 0.5 to 1.5
- conv_mixer: float32 [4, 8192], P(None, 'tp'), may hold values from -3 to 3
- conv_input: float32 [4, 1024], P(None, 'tp'), may hold values from -3 to 3
- conv_output: float32 [4, 1024], P(None, 'tp'), may hold values from -3 to 3
- norm_gain: float32 [8192], P('tp'), may hold values from 0.5 to 1.5
- queries: bfloat16 [1024, 8192], P('seq', 'tp'), may hold values from -5 to 5
- keys: bfloat16 [1024, 1024], P('seq', 'tp'), may hold values from -5 to 5
- values: bfloat16 [1024, 1024], P('seq', 'tp'), may hold values from -6 to 6
Outputs:
- mixer_out: bfloat16 [1024, 8192], P('seq', 'tp')
- attention_out: bfloat16 [1024, 8192], P('seq', 'tp')
All inputs are finite; a program needn't handle non-finite values.
Results may differ from a plain program's by a relative error of at most 0.007.
Values may be sent and summed in bfloat16 or wider, within the bound.
A program may use at most 192 MiB of HBM per device.

v0:
```python
import math

import jax
import jax.numpy as jnp
from jax import lax
from jax.sharding import PartitionSpec as P

MH = 128
P_SIZE = 64
STATE = 128
HD = 128
CONV = 4


HIGHEST = lax.Precision.HIGHEST
norm_epsilon = 1e-05
lowest_score = -1e30


def from_behind(value, axis, by):
    size = lax.axis_size(axis)
    pairs = [(i, i + by) for i in range(size) if 0 <= i + by < size]
    return lax.ppermute(value, axis, pairs)


def carried_in(value, axis, join, neutral):
    count, mine = (lax.axis_size(axis), lax.axis_index(axis))
    pieces = jax.tree.map(lambda part: lax.all_gather(part, axis), value)
    subtotal = jax.tree.map(
        lambda part, zero: jnp.full_like(part, 0) + jnp.asarray(zero, part.dtype), value, neutral
    )

    def turn(position, subtotal):
        longer = join(subtotal, jax.tree.map(lambda part: part[position], pieces))
        return jax.tree.map(lambda new, old: jnp.where(position < mine, new, old), longer, subtotal)

    return lax.fori_loop(0, count - 1, turn, subtotal)


def conv_silu(raw_rows, weights, history):
    padded = jnp.concatenate([history, raw_rows], axis=0).astype(jnp.float32)
    length = raw_rows.shape[0]
    summed = jnp.zeros((length, raw_rows.shape[1]), jnp.float32)
    for offset in range(weights.shape[0]):
        summed = summed + weights[offset][None, :] * padded[offset : offset + length]
    return jax.nn.silu(summed)


def ssd_block(signal, b_state, c_state, step_size, rates, carried):
    group_heads = signal.shape[1] // b_state.shape[1]
    log_decay = jnp.cumsum(-step_size * rates[None, :], axis=0)
    length = signal.shape[0]
    places = jnp.arange(length, dtype=jnp.int32)
    causal = (places[:, None] >= places[None, :])[:, :, None]
    spread = jnp.where(causal, log_decay[:, None, :] - log_decay[None, :, :], 0.0)
    decays = jnp.where(causal, jnp.exp(spread), 0.0)
    coupling = jnp.einsum("tgn,sgn->gts", c_state, b_state, precision=HIGHEST)
    coupling = jnp.repeat(coupling, group_heads, axis=0)
    mixing = jnp.transpose(decays, (2, 0, 1)) * coupling
    scaled = signal * step_size[:, :, None]
    output = jnp.einsum("hts,shp->thp", mixing, scaled, precision=HIGHEST)
    b_heads = jnp.repeat(b_state, group_heads, axis=1)
    c_heads = jnp.repeat(c_state, group_heads, axis=1)
    output = output + jnp.exp(log_decay)[:, :, None] * jnp.einsum(
        "thn,hpn->thp", c_heads, carried, precision=HIGHEST
    )
    closing = jnp.exp(log_decay[-1][None, :] - log_decay)
    weighted = scaled * closing[:, :, None]
    updated = jnp.exp(log_decay[-1])[:, None, None] * carried + jnp.einsum(
        "shp,shn->hpn", weighted, b_heads, precision=HIGHEST
    )
    return (output, updated, log_decay, c_heads)


def combine_states(earlier, later):
    return (earlier[0] * later[0], later[0][:, None, None] * earlier[1] + later[1])


def attend_update(carry, query_block, query_start, key_block, value_block, key_start):
    maxima, totals, accum = carry
    kv_heads = key_block.shape[1] // HD
    grouped = query_block.shape[1] // HD // kv_heads
    query_rows = query_block.shape[0]
    key_rows = key_block.shape[0]
    query_four = query_block.reshape(query_rows, kv_heads, grouped, HD)
    key_three = key_block.reshape(key_rows, kv_heads, HD)
    value_three = value_block.reshape(key_rows, kv_heads, HD)
    scores = jnp.einsum("qhgd,khd->hgqk", query_four, key_three, preferred_element_type=jnp.float32)
    scores = scores * (1.0 / math.sqrt(HD))
    query_places = query_start + jnp.arange(query_rows, dtype=jnp.int32)
    key_places = key_start + jnp.arange(key_rows, dtype=jnp.int32)
    allowed = key_places[None, :] <= query_places[:, None]
    masked = jnp.where(allowed, scores, lowest_score)
    newmax = jnp.maximum(maxima, jnp.max(masked, axis=-1))
    probs = jnp.where(allowed, jnp.exp(masked - newmax[..., None]), 0.0)
    factor = jnp.exp(maxima - newmax)
    totals = totals * factor + jnp.sum(probs, axis=-1)
    rounded = probs.astype(jnp.bfloat16)
    product = jnp.einsum("hgqk,khd->hgqd", rounded, value_three, preferred_element_type=jnp.float32)
    accum = accum * factor[..., None] + product
    return (newmax, totals, accum)


def finish(carry):
    maxima, totals, accum = carry
    result = accum / totals[..., None]
    result = jnp.transpose(result, (2, 0, 1, 3))
    return result.reshape(result.shape[0], -1).astype(jnp.bfloat16)


def mixer_local(
    mixer_input,
    gate_input,
    input_matrix,
    output_matrix,
    step_raw,
    step_bias,
    decay_rate,
    skip_weight,
    conv_mixer,
    conv_input,
    conv_output,
    norm_gain,
):
    reach = CONV - 1
    history = from_behind(
        (mixer_input[-reach:], input_matrix[-reach:], output_matrix[-reach:]), "seq", 1
    )
    length = mixer_input.shape[0]
    heads = mixer_input.shape[1] // P_SIZE
    groups = input_matrix.shape[1] // STATE
    signal = conv_silu(mixer_input, conv_mixer, history[0]).reshape(length, heads, P_SIZE)
    b_state = conv_silu(input_matrix, conv_input, history[1]).reshape(length, groups, STATE)
    c_state = conv_silu(output_matrix, conv_output, history[2]).reshape(length, groups, STATE)
    step_size = jax.nn.softplus(step_raw + step_bias[None, :])
    carried = jnp.zeros((heads, P_SIZE, STATE), jnp.float32)
    output, carried, log_decay, c_heads = ssd_block(
        signal, b_state, c_state, step_size, decay_rate, carried
    )
    offset_log = log_decay[-1]
    device_decay = jnp.exp(offset_log)
    identity = (jnp.ones((heads,), jnp.float32), jnp.zeros((heads, P_SIZE, STATE), jnp.float32))
    prefix_decay, entering = carried_in((device_decay, carried), "seq", combine_states, identity)
    mixed = output
    mixed = mixed + jnp.exp(log_decay)[:, :, None] * jnp.einsum(
        "thn,hpn->thp", c_heads, entering, precision=HIGHEST
    )
    mixed = mixed + skip_weight[None, :, None] * signal
    gated = mixed.reshape(length, heads * P_SIZE) * jax.nn.silu(gate_input.astype(jnp.float32))
    squares = lax.psum(jnp.sum(gated * gated, axis=1), "tp")
    scaling = lax.rsqrt(squares / (MH * P_SIZE) + norm_epsilon)
    return (gated * scaling[:, None] * norm_gain[None, :]).astype(jnp.bfloat16)


def attend_local(queries, keys, values):
    length = queries.shape[0]
    half_len = length // 2
    device = lax.axis_index("seq")
    own_start = device * length
    near_rows = queries[:half_len]
    far_rows = queries[half_len:]
    far_start = own_start + half_len
    kv_heads = keys.shape[1] // HD
    grouped = queries.shape[1] // HD // kv_heads

    def fresh():
        return (
            jnp.full((kv_heads, grouped, half_len), lowest_score, jnp.float32),
            jnp.zeros((kv_heads, grouped, half_len), jnp.float32),
            jnp.zeros((kv_heads, grouped, half_len, HD), jnp.float32),
        )

    key_piece = lax.all_gather(keys, "seq", axis=0, tiled=True)
    value_piece = lax.all_gather(values, "seq", axis=0, tiled=True)
    span = math.gcd(key_piece.shape[0], 512)

    def visit(position, inner):
        key_start = position * span
        key_block = lax.dynamic_slice_in_dim(key_piece, position * span, span, 0)
        value_block = lax.dynamic_slice_in_dim(value_piece, position * span, span, 0)
        near_state = lax.cond(
            key_start <= own_start + half_len - 1,
            lambda carry_in: attend_update(
                carry_in, near_rows, own_start, key_block, value_block, key_start
            ),
            lambda carry_in: carry_in,
            inner[0],
        )
        far_state = lax.cond(
            key_start <= far_start + half_len - 1,
            lambda carry_in: attend_update(
                carry_in, far_rows, far_start, key_block, value_block, key_start
            ),
            lambda carry_in: carry_in,
            inner[1],
        )
        return (near_state, far_state)

    near_state, far_state = lax.fori_loop(0, key_piece.shape[0] // span, visit, (fresh(), fresh()))
    near_out = finish(near_state)
    far_out = finish(far_state)
    return jnp.concatenate([near_out, far_out], axis=0)


def shards(
    mixer_input,
    gate_input,
    input_matrix,
    output_matrix,
    step_raw,
    step_bias,
    decay_rate,
    skip_weight,
    conv_mixer,
    conv_input,
    conv_output,
    norm_gain,
    queries,
    keys,
    values,
):
    mixer_out = mixer_local(
        mixer_input,
        gate_input,
        input_matrix,
        output_matrix,
        step_raw,
        step_bias,
        decay_rate,
        skip_weight,
        conv_mixer,
        conv_input,
        conv_output,
        norm_gain,
    )
    attention_out = attend_local(queries, keys, values)
    return (mixer_out, attention_out)


def solution(mesh):
    placed = (
        P("seq", "tp"),
        P("seq", "tp"),
        P("seq", "tp"),
        P("seq", "tp"),
        P("seq", "tp"),
        P("tp"),
        P("tp"),
        P("tp"),
        P(None, "tp"),
        P(None, "tp"),
        P(None, "tp"),
        P("tp"),
        P("seq", "tp"),
        P("seq", "tp"),
        P("seq", "tp"),
    )
    return jax.shard_map(
        shards,
        mesh=mesh,
        in_specs=placed,
        out_specs=(P("seq", "tp"), P("seq", "tp")),
        check_vma=False,
    )
```

profile of v0, /device:TPU:0, one launch (start us, length us, event | category | flops | bytes accessed | tf_op | source)
XLA Modules:
  0.0 195.7 jit_solution(2832817880252350964)
XLA Ops:
  7.2 0.7 slice.111
  7.9 4.9 %collective-permute-start.2 = (bf16[3,256]{1,0:T(4,128)(2,1)S(1)}, bf16[3,256]{1,0:T(4,128)(2,1)S(1)}, u32[]{:S(2)}, u32[]{:S(2)}) collective-permute-start(bf16[3,256]{1,0:T(4,128)(2,1)S(1)} %slice.111), channel_id=1, source_target_pairs={{0,4},{4,8},{8,12},{12,16},{16,20},{20,24},{24,28},{1,5},{5,9},{9,... | collective-permute-start | bytes 4616 | tf_op jit(solution)/shard_map/ppermute | solution.py:23
  12.8 0.8 slice.93
  13.6 3.4 %collective-permute-start = (bf16[3,2048]{1,0:T(4,128)(2,1)S(1)}, bf16[3,2048]{1,0:T(4,128)(2,1)S(1)}, u32[]{:S(2)}, u32[]{:S(2)}) collective-permute-start(bf16[3,2048]{1,0:T(4,128)(2,1)S(1)} %slice.93), channel_id=1, source_target_pairs={{0,4},{4,8},{8,12},{12,16},{16,20},{20,24},{24,28},{1,5},{5,9},{9,... | collective-permute-start | bytes 36872 | tf_op jit(solution)/shard_map/ppermute | solution.py:23
  17.0 0.8 negate_multiply_fusion
  18.7 0.8 fusion.64
  19.5 1.0 fusion.62
  20.5 0.6 fusion.61
  21.2 0.9 maximum_convert_fusion.2
  22.8 1.2 maximum_convert_fusion
  25.2 3.1 %convolution_add_fusion.2 = f32[32,64,128]{2,1,0:T(8,128)} fusion(f32[128,32,128]{2,0,1:T(8,128)S(1)} %bitcast.126, f32[128,32,64]{0,2,1:T(8,128)S(1)} %bitcast.122, f32[128,32]{0,1:T(8,128)S(1)} %copy.50, f32[32]{0:T(128)S(1)} %exponential_multiply_fusion, f32[128,32]{0,1:T(8,128)S(1)} %get-tuple-element.612), kind=kOutput, calls=%fused_computation.52 | convolution fusion | flops 403439616 | bytes 4227200 | tf_op jit(solution)/shard_map/shp,shn->hpn/dot_general | solution.py:69
  28.4 1.3 slice.102
  29.7 4.0 %collective-permute-start.1 = (bf16[3,256]{1,0:T(4,128)(2,1)}, bf16[3,256]{1,0:T(4,128)(2,1)}, u32[]{:S(2)}, u32[]{:S(2)}) collective-permute-start(bf16[3,256]{1,0:T(4,128)(2,1)} %slice.102), channel_id=1, source_target_pairs={{0,4},{4,8},{8,12},{12,16},{16,20},{20,24},{24,28},{1,5},{5,9},{9,... | collective-permute-start | bytes 4616 | tf_op jit(solution)/shard_map/ppermute | solution.py:23
  33.7 35.8 %all_gather.19 = bf16[1024,256]{1,0:T(8,128)(2,1)} all-gather(bf16[128,256]{1,0:T(8,128)(2,1)S(1)} %copy-done.12), channel_id=1, replica_groups=mesh['seq'=8,'tp'=4] {'seq'}, dimensions={0}, use_global_device_ids=true | all-gather | bytes 589824 | tf_op jit(solution)/shard_map/all_gather | solution.py:173
  69.6 35.9 %all_gather.20 = bf16[1024,256]{1,0:T(8,128)(2,1)} all-gather(bf16[128,256]{1,0:T(8,128)(2,1)S(1)} %copy-done.13), channel_id=1, replica_groups=mesh['seq'=8,'tp'=4] {'seq'}, dimensions={0}, use_global_device_ids=true | all-gather | bytes 589824 | tf_op jit(solution)/shard_map/all_gather | solution.py:174
  105.5 0.8 broadcast.80
  106.4 0.8 broadcast.80.clone
  107.2 12.2 %while.40 = (s32[]{:T(128)}, f32[2,8,64]{2,1,0:T(8,128)S(1)}, f32[2,8,64]{2,1,0:T(8,128)S(1)}, f32[2,8,64,128]{3,2,1,0:T(8,128)}, f32[2,8,64]{2,1,0:T(8,128)S(1)...) while((s32[]{:T(128)}, f32[2,8,64]{2,1,0:T(8,128)S(1)}, ...), condition=%wide.region_14.15_spmd, body=%wide.region_5.14_spmd.sunk | while | flops 551097472 | bytes 20850180 | solution.py:199
  107.2 1.1 constant_dynamic-slice_fusion.3
  108.3 5.8 %conditional.4 = ((f32[2,8,64]{2,1,0:T(8,128)S(1)}, f32[2,8,64]{2,1,0:T(8,128)S(1)}, f32[2,8,64,128]{3,2,1,0:T(8,128)})) conditional(s32[]{:T(128)} %convert_element_type.102, (f32[2,8,64]{2,1,0:T(8,128)S(1)}, f32[2,8,64]{2,1,0:T(8,128)S(1)}, f32[2,8,64,128]{3,2,1,0:T(8,128)}) %tuple.107, (s32[]{:T(128)}, s32[]{:T(128)}, ...), branch_computations={%region_6.6_spmd, %region_7.9_spmd} | conditional | flops 275548736 | bytes 9900584 | solution.py:181
  108.5 0.8 reshape.102
  109.2 1.5 fusion
  110.8 0.7 fusion.2
  111.5 2.6 %convolution_add_fusion = f32[2,8,64,128]{3,2,1,0:T(8,128)} fusion(f32[2,512,64,8]{1,2,3,0:T(8,128)S(1)} %get-tuple-element.614, f32[2,8,64]{2,1,0:T(8,128)S(1)} %max.10, pred[64,512]{1,0:T(8,128)(4,1)S(1)} %broadcast_compare_fusion, f32[2,8,64,128]{3,2,1,0:T(8,128)} %get-tuple-element.505, bf16[512,2,128,1]{2,1,0,3:T(2,128)(2,1)S(1)} %bitcast.127, ...), kind=kOutput, calls=%fused_computation.5 | convolution fusion | flops 137101312 | bytes 3448832 | tf_op jit(solution)/shard_map/while/body/eval_jaxpr/cond/branch_1_fun/hgqk,khd->hgqd/dot_general | solution.py:99
  114.1 4.2 %conditional.5 = ((f32[2,8,64]{2,1,0:T(8,128)S(1)}, f32[2,8,64]{2,1,0:T(8,128)S(1)}, f32[2,8,64,128]{3,2,1,0:T(8,128)})) conditional(s32[]{:T(128)} %convert_element_type.103, (f32[2,8,64]{2,1,0:T(8,128)S(1)}, f32[2,8,64]{2,1,0:T(8,128)S(1)}, f32[2,8,64,128]{3,2,1,0:T(8,128)}) %tuple.109, (s32[]{:T(128)}, s32[]{:T(128)}, ...), branch_computations={%region_10.10_spmd, %region_11.13_spmd} | conditional | flops 275548736 | bytes 9900584 | solution.py:189
  114.9 0.7 fusion.17
  115.7 2.6 %convolution_add_fusion.1 = f32[2,8,64,128]{3,2,1,0:T(8,128)} fusion(f32[2,512,64,8]{1,2,3,0:T(8,128)S(1)} %get-tuple-element.616, f32[2,8,64]{2,1,0:T(8,128)S(1)} %max.11, pred[64,512]{1,0:T(8,128)(4,1)S(1)} %broadcast_compare_fusion.1, f32[2,8,64,128]{3,2,1,0:T(8,128)} %get-tuple-element.513, bf16[512,2,128,1]{2,1,0,3:T(2,128)(2,1)S(1)} %bitcast.128, ...), kind=kOutput, calls=%fused_computation.27 | convolution fusion | flops 137101312 | bytes 3448832 | tf_op jit(solution)/shard_map/while/body/eval_jaxpr/cond/branch_1_fun/hgqk,khd->hgqd/dot_general | solution.py:99
  118.3 1.1 constant_dynamic-slice_fusion.3
  119.5 1.6 fusion.50
  121.6 0.8 pad_maximum_fusion
  122.6 27.6 %all-gather.1 = f32[8,1,32]{2,1,0:T(1,128)S(1)} all-gather(f32[1,1,32]{2,1,0:T(1,128)S(1)} %copy-done.25), channel_id=1, replica_groups=mesh['seq'=8,'tp'=4] {'seq'}, dimensions={0}, use_global_device_ids=true | all-gather | bytes 1152 | tf_op jit(solution)/shard_map/all_gather | solution.py:28
  150.3 0.7 maximum_convert_fusion.1
  151.6 1.7 bitcast_multiply_fusion
  153.6 5.1 %fusion.32 = f32[128,32,64]{0,2,1:T(8,128)} fusion(f32[128,32,128]{2,0,1:T(8,128)S(1)} %bitcast.120, f32[128,32]{0,1:T(8,128)S(1)} %copy.48), kind=kOutput, calls=%fused_computation.54 | convolution fusion | flops 402915328 | bytes 3162112 | tf_op jit(solution)/shard_map/thn,hpn->thp/dot_general | solution.py:64
  158.8 2.8 %all-gather.4.cloned.1.call-done = f32[256,64,128]{2,1,0:T(8,128)} async-done(((f32[32,64,128]{2,1,0:T(8,128)}), f32[256,64,128]{2,1,0:T(8,128)}) %all-gather.4.cloned.1.call-update) | async-done | bytes 8388624 | tf_op jit(solution)/shard_map/all_gather | solution.py:28
  161.6 10.5 %while.41 = (s32[]{:T(128)}, f32[32,64,128]{2,1,0:T(8,128)S(1)}, s32[]{:T(128)}, f32[8,32]{1,0:T(8,128)S(1)}, f32[8,32,64,128]{3,2,1,0:T(8,128)}, /*index=5*/s32[]{:T(128)}, s32[]{:T(128)}) while((s32[]{:T(128)}, f32[32,64,128]{2,1,0:T(8,128)S(1)}, s32[]{:T(128)}, f32[8,32]{1,0:T(8,128)S(1)}, f32[8,32,64,128]{3,2,1,0:T(8,128)}, ...), condition=%wide.region_2.3_spmd.clone, body=%wide.region_1.2_spmd.clone.sunk | while | flops 1048580 | bytes 3146225 | solution.py:37
  161.6 1.5 fusion.71
  163.1 1.5 fusion.71
  164.6 1.5 fusion.71
  166.1 1.5 fusion.71
  167.6 1.5 fusion.71
  169.1 1.5 fusion.71
  170.6 1.5 fusion.71
  172.1 4.2 %fusion.31 = f32[128,32,64]{0,2,1:T(8,128)S(1)} fusion(f32[32,64,128]{2,1,0:T(8,128)S(1)} %get-tuple-element.544, f32[128,32,128]{2,0,1:T(8,128)S(1)} %bitcast.121, f32[128,32]{0,1:T(8,128)S(1)} %copy.48), kind=kOutput, calls=%fused_computation.51 | convolution fusion | flops 402915328 | bytes 4210688 | tf_op jit(solution)/shard_map/thn,hpn->thp/dot_general | solution.py:145
  176.4 4.2 %fusion.35 = f32[128,32,64]{0,2,1:T(8,128)S(1)} fusion(f32[128,32,64]{0,2,1:T(8,128)S(1)} %fusion.31, f32[128,32,64]{0,2,1:T(8,128)S(1)} %copy-done.3, f32[32,128,128]{2,1,0:T(8,128)S(1)} %copy-done.2, f32[128,32,64]{0,2,1:T(8,128)S(1)} %bitcast.123, f32[32]{0:T(128)S(1)} %copy-done.24, f32[128,32]{0,1:T(8,128)S(1)} %copy-done.10), kind=kOutput, calls=%fused_computation.58 | convolution fusion | flops 403963904 | bytes 6307968 | tf_op jit(solution)/shard_map/hts,shp->thp/dot_general | solution.py:61
  180.9 0.7 copy-done.6
  182.0 5.7 %psum.7 = f32[128]{0:T(128)S(1)} all-reduce(f32[128]{0:T(128)S(1)} %multiply_reduce_fusion), channel_id=1, replica_groups=mesh['seq'=8,'tp'=4] {'tp'}, use_global_device_ids=true, to_apply=%region_4.5 | all-reduce | flops 128 | bytes 1024 | tf_op jit(solution)/shard_map/psum | solution.py:150
  187.7 1.2 multiply_convert_fusion
  (112 shorter events, 6.3 us)
Async XLA Ops:
  7.2 154.4 %all-gather.4.cloned.1.call-start = ((), (), s32[]{:S(2)}) async-start(), calls=%async_computation | async-start | bytes 9437184 | tf_op jit(solution)/shard_map/all_gather | solution.py:28
  7.9 13.3 %collective-permute-start.2 = (bf16[3,256]{1,0:T(4,128)(2,1)S(1)}, bf16[3,256]{1,0:T(4,128)(2,1)S(1)}, u32[]{:S(2)}, u32[]{:S(2)}) collective-permute-start(bf16[3,256]{1,0:T(4,128)(2,1)S(1)} %slice.111), channel_id=1, source_target_pairs={{0,4},{4,8},{8,12},{12,16},{16,20},{20,24},{24,28},{1,5},{5,9},{9,... | collective-permute-start | bytes 4616 | tf_op jit(solution)/shard_map/ppermute | solution.py:23
  13.6 9.2 %collective-permute-start = (bf16[3,2048]{1,0:T(4,128)(2,1)S(1)}, bf16[3,2048]{1,0:T(4,128)(2,1)S(1)}, u32[]{:S(2)}, u32[]{:S(2)}) collective-permute-start(bf16[3,2048]{1,0:T(4,128)(2,1)S(1)} %slice.93), channel_id=1, source_target_pairs={{0,4},{4,8},{8,12},{12,16},{16,20},{20,24},{24,28},{1,5},{5,9},{9,... | collective-permute-start | bytes 36872 | tf_op jit(solution)/shard_map/ppermute | solution.py:23
  17.8 7.4 %copy-start.9 = (f32[128,32]{0,1:T(8,128)}, f32[128,32]{0,1:T(8,128)S(1)}, u32[]{:S(2)}) copy-start(f32[128,32]{0,1:T(8,128)S(1)} %get-tuple-element.612) | copy-start | bytes 49156
  19.5 5.1 %copy-start.15 = (f32[1,256]{1,0:T(1,128)}, f32[1,256]{1,0:T(1,128)S(1)}, u32[]{:S(2)}) copy-start(f32[1,256]{1,0:T(1,128)S(1)} %get-tuple-element.633) | copy-start | bytes 3076
  19.5 5.1 %copy-start.17 = (f32[1,256]{1,0:T(1,128)}, f32[1,256]{1,0:T(1,128)S(1)}, u32[]{:S(2)}) copy-start(f32[1,256]{1,0:T(1,128)S(1)} %get-tuple-element.634) | copy-start | bytes 3076
  19.5 5.1 %copy-start.19 = (f32[1,256]{1,0:T(1,128)}, f32[1,256]{1,0:T(1,128)S(1)}, u32[]{:S(2)}) copy-start(f32[1,256]{1,0:T(1,128)S(1)} %get-tuple-element.635) | copy-start | bytes 3076
  19.5 5.1 %copy-start.21 = (f32[1,256]{1,0:T(1,128)}, f32[1,256]{1,0:T(1,128)S(1)}, u32[]{:S(2)}) copy-start(f32[1,256]{1,0:T(1,128)S(1)} %get-tuple-element.636) | copy-start | bytes 3076
  22.1 0.7 copy-start.4
  25.0 3.4 %copy-start = (f32[128,2048]{0,1:T(8,128)}, f32[128,2048]{0,1:T(8,128)S(1)}, u32[]{:S(2)}) copy-start(f32[128,2048]{0,1:T(8,128)S(1)} %copy.42) | copy-start | bytes 3145732
  25.2 8.5 %copy-start.12 = (bf16[128,256]{1,0:T(8,128)(2,1)S(1)}, bf16[128,256]{1,0:T(8,128)(2,1)}, u32[]{:S(2)}) copy-start(bf16[128,256]{1,0:T(8,128)(2,1)} %param.36) | copy-start | bytes 196612
  25.2 44.4 %copy-start.13 = (bf16[128,256]{1,0:T(8,128)(2,1)S(1)}, bf16[128,256]{1,0:T(8,128)(2,1)}, u32[]{:S(2)}) copy-start(bf16[128,256]{1,0:T(8,128)(2,1)} %param.37) | copy-start | bytes 196612
  28.4 77.1 %copy-start.7 = (bf16[128,2048]{1,0:T(8,128)(2,1)S(1)}, bf16[128,2048]{1,0:T(8,128)(2,1)}, u32[]{:S(2)}) copy-start(bf16[128,2048]{1,0:T(8,128)(2,1)} %param.35) | copy-start | bytes 1572868
  29.7 120.5 %collective-permute-start.1 = (bf16[3,256]{1,0:T(4,128)(2,1)}, bf16[3,256]{1,0:T(4,128)(2,1)}, u32[]{:S(2)}, u32[]{:S(2)}) collective-permute-start(bf16[3,256]{1,0:T(4,128)(2,1)} %slice.102), channel_id=1, source_target_pairs={{0,4},{4,8},{8,12},{12,16},{16,20},{20,24},{24,28},{1,5},{5,9},{9,... | collective-permute-start | bytes 4616 | tf_op jit(solution)/shard_map/ppermute | solution.py:23
  119.4 2.2 %copy-start.23 = (f32[4,256]{1,0:T(4,128)S(1)}, f32[4,256]{1,0:T(4,128)}, u32[]{:S(2)}) copy-start(f32[4,256]{1,0:T(4,128)} %param.33) | copy-start | bytes 12292
  119.4 3.1 %copy-start.8 = (f32[128,32]{1,0:T(8,128)S(1)}, f32[128,32]{1,0:T(8,128)}, u32[]{:S(2)}) copy-start(f32[128,32]{1,0:T(8,128)} %get-tuple-element.621) | copy-start | bytes 49156
  119.4 3.2 %copy-start.25 = (f32[1,1,32]{2,1,0:T(1,128)S(1)}, f32[1,1,32]{2,1,0:T(1,128)}, u32[]{:S(2)}) copy-start(f32[1,1,32]{2,1,0:T(1,128)} %get-tuple-element.624) | copy-start | bytes 388
  119.4 30.8 %copy-start.11 = (bf16[128,256]{1,0:T(8,128)(2,1)S(1)}, bf16[128,256]{1,0:T(8,128)(2,1)}, u32[]{:S(2)}) copy-start(bf16[128,256]{1,0:T(8,128)(2,1)} %param.26) | copy-start | bytes 196612
  121.0 29.9 %copy-start.5 = (f32[131,256]{1,0:T(8,128)S(1)}, f32[131,256]{1,0:T(8,128)}, u32[]{:S(2)}) copy-start(f32[131,256]{1,0:T(8,128)} %copy-done.4) | copy-start | bytes 402436
  121.1 29.9 %copy-start.16 = (f32[1,256]{1,0:T(1,128)S(1)}, f32[1,256]{1,0:T(1,128)}, u32[]{:S(2)}) copy-start(f32[1,256]{1,0:T(1,128)} %copy-done.15) | copy-start | bytes 3076
  121.1 29.9 %copy-start.18 = (f32[1,256]{1,0:T(1,128)S(1)}, f32[1,256]{1,0:T(1,128)}, u32[]{:S(2)}) copy-start(f32[1,256]{1,0:T(1,128)} %copy-done.17) | copy-start | bytes 3076
  121.1 29.9 %copy-start.20 = (f32[1,256]{1,0:T(1,128)S(1)}, f32[1,256]{1,0:T(1,128)}, u32[]{:S(2)}) copy-start(f32[1,256]{1,0:T(1,128)} %copy-done.19) | copy-start | bytes 3076
  121.1 29.9 %copy-start.22 = (f32[1,256]{1,0:T(1,128)S(1)}, f32[1,256]{1,0:T(1,128)}, u32[]{:S(2)}) copy-start(f32[1,256]{1,0:T(1,128)} %copy-done.21) | copy-start | bytes 3076
  161.6 14.7 %copy-start.24 = (f32[32]{0:T(128)S(1)}, f32[32]{0:T(128)}, u32[]{:S(2)}) copy-start(f32[32]{0:T(128)} %param.30) | copy-start | bytes 388
  172.1 4.2 %copy-start.1 = (f32[128,2048]{0,1:T(8,128)S(1)}, f32[128,2048]{0,1:T(8,128)}, u32[]{:S(2)}) copy-start(f32[128,2048]{0,1:T(8,128)} %copy-done) | copy-start | bytes 3145732
  172.1 4.2 %copy-start.2 = (f32[32,128,128]{2,1,0:T(8,128)S(1)}, f32[32,128,128]{2,1,0:T(8,128)}, u32[]{:S(2)}) copy-start(f32[32,128,128]{2,1,0:T(8,128)} %bitcast_multiply_fusion) | copy-start | bytes 6291460
  172.1 4.2 %copy-start.3 = (f32[128,32,64]{0,2,1:T(8,128)S(1)}, f32[128,32,64]{0,2,1:T(8,128)}, u32[]{:S(2)}) copy-start(f32[128,32,64]{0,2,1:T(8,128)} %fusion.32) | copy-start | bytes 3145732
  172.1 4.2 %copy-start.10 = (f32[128,32]{0,1:T(8,128)S(1)}, f32[128,32]{0,1:T(8,128)}, u32[]{:S(2)}) copy-start(f32[128,32]{0,1:T(8,128)} %copy-done.9) | copy-start | bytes 49156
  180.6 1.0 copy-start.6
  180.6 7.1 %copy-start.14 = (f32[2048]{0:T(1024)S(1)}, f32[2048]{0:T(1024)}, u32[]{:S(2)}) copy-start(f32[2048]{0:T(1024)} %param.34) | copy-start | bytes 24580
Sparse Core Ops, SparseCore 0:
  28.5 133.0 all-gather.3
where the time goes:
time: 197 us; the launch traced here: 196 us
  blocking collectives  105 us (53%)
  matrix products  24.4 us (12%)
  other arithmetic  22.8 us (12%)
  between operations  14.6 us (7%)
  local copies, waits for them, and re-layouts  13.4 us (7%)
  starting transfers between devices  12.4 us (6%)
  waiting for transfers between devices  2.85 us (1%)
    all_gather x1, blocking collectives, attend_local(): value_piece = lax.all_gather(values, 'seq', axis=0, tiled=True)  35.9 us
    all_gather x1, blocking collectives, attend_local(): key_piece = lax.all_gather(keys, 'seq', axis=0, tiled=True)  35.8 us
    all_gather x1, blocking collectives, carried_in(): pieces = jax.tree.map(lambda part: lax.all_gather(part, axis), value)  27.6 us
    ppermute x3, starting transfers between devices, from_behind(): return lax.ppermute(value, axis, pairs)  12.3 us
    select_n x7, other arithmetic, turn(): jnp.where(position < mine, new, old)  10.2 us
    psum x1, blocking collectives, mixer_local(): squares = lax.psum(jnp.sum(gated * gated, axis=1), 'tp')  5.67 us
    dot_general x2, matrix products, attend_update(): jnp.einsum('hgqk,khd->hgqd', rounded, value_three, preferred_element_type...  5.16 us
    dot_general x1, matrix products, ssd_block(): jnp.einsum('thn,hpn->thp', c_heads, carried, precision=HIGHEST)  5.15 us
  transfers between devices with their start and end apart: 4, of which 1 were waited for; matrix products, arithmetic and copies ran while one was open for 17% of the time, Pallas kernels for 0%

commit v1 on v0

v1 whole, which is shorter than its diff:
```python
import functools
import math

import jax
import jax.numpy as jnp
from jax import lax
from jax.experimental import pallas as pl
from jax.experimental.pallas import tpu as pltpu
from jax.sharding import PartitionSpec as P


P_SIZE = 64
STATE = 128
HD = 128
COLS = 2
CHUNKS = 4
HALO = 16
EPS = 1e-05
LOWEST = -1e30
MESH = pl.DeviceIdType.MESH
F32 = jnp.float32
BF16 = jnp.bfloat16


def dot(a, b, ca=1, cb=0):
    return lax.dot_general(a, b, (((ca,), (cb,)), ((), ())), preferred_element_type=F32)


def pieces_of(a, terms):
    out = []
    for _ in range(terms):
        head = a.astype(BF16)
        out.append(head)
        a = a - head.astype(F32)
    return out


def silu(a):
    return a / (1.0 + jnp.exp(-a))


def kernel(
    n, tp, inner,
    x_ref, gate_ref, b_ref, c_ref, step_ref, bias_ref, rate_ref, skip_ref,
    cx_ref, cb_ref, cc_ref, gain_ref, q_ref, k_ref, v_ref,
    mix_out, att_out,
    hx, hb, hc, padx, padb, sig, wgt, scl, ex, bst, cst,
    s_buf, r1, e_in, e_out, p_out, ent, p_in, dec_own, dec_par,
    kbuf, vbuf, qs, acc, m_sc, l_sc, ybuf, sq_own, sq_in,
    halo_s, halo_r, dec_s, dec_r, p1_s, p1_r, p2_s, p2_r, p3_s, p3_r,
    kc_s, kc_r, kp_s, kp_r, kl_s, sq_s, sq_r,
):
    me = lax.axis_index("seq")
    mytp = lax.axis_index("tp")
    rows = n // COLS
    row = me // COLS
    col = me % COLS
    other = 1 - col
    partner = row * COLS + other
    length, width = x_ref.shape
    half = width // 2
    cw = half // CHUNKS
    groups = b_ref.shape[1] // STATE
    gwidth = width // groups
    heads = width // P_SIZE
    kvh = k_ref.shape[1] // HD
    qper = q_ref.shape[1] // HD // kvh

    barrier = pltpu.get_barrier_semaphore()

    @pl.loop(1, n)
    def _(d):
        pl.semaphore_signal(barrier, inc=1, device_id={"seq": (me + d) % n}, device_id_type=MESH)

    for d in range(1, tp):
        pl.semaphore_signal(
            barrier, inc=1, device_id={"tp": (mytp + d) % tp}, device_id_type=MESH
        )

    pre = step_ref[...] + bias_ref[...]
    dt = jnp.maximum(pre, 0.0) + jnp.log1p(jnp.exp(-jnp.abs(pre)))
    a = -dt * rate_ref[...]
    ri = lax.broadcasted_iota(jnp.int32, (length, length), 0)
    ci = lax.broadcasted_iota(jnp.int32, (length, length), 1)
    lower = (ri >= ci).astype(F32).astype(BF16)
    upper = (ri <= ci).astype(F32).astype(BF16)
    apieces = pieces_of(a, 3)
    logd = sum(dot(lower, p) for p in apieces)
    logt = sum(dot(p, upper, 0, 0) for p in apieces)
    last = logd[length - 1 : length, :]
    closing = jnp.exp(last - logd)
    hi = lax.broadcasted_iota(jnp.int32, (heads, width), 0)
    wi = lax.broadcasted_iota(jnp.int32, (heads, width), 1)
    spread = (wi // P_SIZE == hi).astype(F32).astype(BF16)
    many = jnp.concatenate([dt, dt * closing, jnp.exp(logd)], axis=0)
    wide = sum(dot(p, spread) for p in pieces_of(many, 2))
    dtx, wx, elx = wide[:length], wide[length : 2 * length], wide[2 * length :]
    skipx = sum(dot(p, spread) for p in pieces_of(jnp.broadcast_to(skip_ref[...], (8, heads)), 3))[:1]
    for h in range(2):
        cut = slice(h * half, (h + 1) * half)
        ex[h] = elx[:, cut]
        scl[h] = dtx[:, cut]
        sig[h] = wx[:, cut]
        dec_own[h] = elx[length - 1 : length, cut]

    pl.semaphore_wait(barrier, n - 1 + tp - 1)

    def halo(dst):
        out = []
        for i, (src, buf) in enumerate(((x_ref, hx), (b_ref, hb), (c_ref, hc))):
            out.append(
                pltpu.make_async_remote_copy(
                    src_ref=src.at[pl.ds(length - HALO, HALO)], dst_ref=buf,
                    send_sem=halo_s.at[i], recv_sem=halo_r.at[i],
                    device_id={"seq": dst}, device_id_type=MESH,
                )
            )
        return out

    @pl.when(me < n - 1)
    def _():
        for cp in halo(me + 1):
            cp.start()

    dec_copy = pltpu.make_async_remote_copy(
        src_ref=dec_own, dst_ref=dec_par, send_sem=dec_s.at[0], recv_sem=dec_r.at[0],
        device_id={"seq": partner}, device_id_type=MESH,
    )
    dec_copy.start()

    def place(c):
        return pl.ds(pl.multiple_of(c * length, length), length)

    def kv_copy(i, dst_row, dst_col, slot_row, slot_col, own, ss, rs, sidx, ridx):
        src = (k_ref, v_ref)[i] if own else (kbuf, vbuf)[i].at[slot_row, place(slot_col)]
        return pltpu.make_async_remote_copy(
            src_ref=src, dst_ref=(kbuf, vbuf)[i].at[slot_row, place(slot_col)],
            send_sem=ss.at[i, sidx], recv_sem=rs.at[i, ridx],
            device_id={"seq": dst_row * COLS + dst_col}, device_id_type=MESH,
        )

    def own_up(i, dst_row):
        return kv_copy(i, dst_row, col, row, col, True, kc_s, kc_r, dst_row, row)

    def own_side(i):
        return kv_copy(i, row, other, row, col, True, kl_s, kp_r, 0, row)

    def relay(i, src_row):
        return kv_copy(i, row, other, src_row, col, False, kp_s, kp_r, src_row, src_row)

    @pl.loop(row + 1, rows)
    def _(dst):
        for i in range(2):
            own_up(i, dst).start()

    for i in range(2):
        own_side(i).start()

    kbuf[row, place(col)] = k_ref[...]
    vbuf[row, place(col)] = v_ref[...]
    for g in range(kvh):
        for h in range(qper):
            at = (g * qper + h) * HD
            qs[g, h * length : (h + 1) * length] = q_ref[:, at : at + HD]

    @pl.when(me > 0)
    def _():
        for cp in halo(me):
            cp.wait_recv()
        padx[:HALO] = hx[...].astype(F32)
        padb[0, :HALO] = hb[...].astype(F32)
        padb[1, :HALO] = hc[...].astype(F32)

    @pl.when(me == 0)
    def _():
        padx[:HALO] = jnp.zeros((HALO, width), F32)
        padb[:, :HALO] = jnp.zeros((2, HALO, b_ref.shape[1]), F32)

    padx[HALO:] = x_ref[...].astype(F32)
    padb[0, HALO:] = b_ref[...].astype(F32)
    padb[1, HALO:] = c_ref[...].astype(F32)
    taps = cx_ref.shape[0]

    def conv(load, w_ref, cut):
        total = None
        for k in range(taps):
            at = HALO - (taps - 1) + k
            term = w_ref[k : k + 1, cut] * load(at)
            total = term if total is None else total + term
        return silu(total)

    for g in range(groups):
        cut = slice(g * STATE, (g + 1) * STATE)
        bst[g] = conv(lambda at: padb[0, at : at + length, cut], cb_ref, cut).astype(BF16)
        cst[g] = conv(lambda at: padb[1, at : at + length, cut], cc_ref, cut).astype(BF16)
    for h in range(2):
        for j in range(CHUNKS):
            cut = slice(h * half + j * cw, h * half + (j + 1) * cw)
            loc = slice(j * cw, (j + 1) * cw)
            s = conv(lambda at: padx[at : at + length, cut], cx_ref, cut)
            wgt[h, j] = (s * sig[h, :, loc]).astype(BF16)
            sig[h, :, loc] = s
            scl[h, :, loc] = s * scl[h, :, loc]

    def group_of(h, j):
        return h * (groups // 2) + (j * cw) // gwidth

    def p1(j):
        return pltpu.make_async_remote_copy(
            src_ref=s_buf.at[other, j], dst_ref=r1.at[j],
            send_sem=p1_s.at[j], recv_sem=p1_r.at[j],
            device_id={"seq": partner}, device_id_type=MESH,
        )

    for j in range(CHUNKS):
        s_buf[other, j] = dot(bst[group_of(other, j)], wgt[other, j], 0, 0).astype(BF16)
        p1(j).start()
    for j in range(CHUNKS):
        s_buf[col, j] = dot(bst[group_of(col, j)], wgt[col, j], 0, 0).astype(BF16)

    @pl.loop(0, row)
    def _(src):
        for i in range(2):
            own = kv_copy(i, row, col, src, col, False, kc_s, kc_r, row, src)
            own.wait_recv()
            relay(i, src).start()

    causal = ri >= ci
    lane = lax.broadcasted_iota(jnp.int32, (length, 128), 1)
    per = 128 // P_SIZE
    for g in range(groups):
        coup = dot(cst[g], bst[g], 1, 1)
        coup = jnp.where(causal, coup, 0.0)
        for t in range(gwidth // 128):
            at = g * gwidth + t * 128
            h, loc = at // half, at % half
            tile = scl[h, :, loc : loc + 128].astype(BF16)
            res = None
            for p in range(per):
                hd = at // P_SIZE + p
                diff = logd[:, hd : hd + 1] - logt[hd : hd + 1, :]
                mixing = (jnp.exp(jnp.minimum(diff, 0.0)) * coup).astype(BF16)
                y = dot(mixing, tile)
                res = y if res is None else jnp.where(lane >= p * P_SIZE, y, res)
            ybuf[h, :, loc : loc + 128] = res + skipx[:, at : at + 128] * sig[h, :, loc : loc + 128]

    scale = math.log2(math.e) / math.sqrt(HD)
    qrows = qper * length

    def attend(lo, hi):
        @pl.loop(lo, hi)
        def _(g):
            m_sc[...] = jnp.full((qrows, 1), LOWEST, F32)
            l_sc[...] = jnp.zeros((qrows, 1), F32)
            acc[...] = jnp.zeros((qrows, HD), F32)
            lanes = pl.ds(pl.multiple_of(g * HD, HD), HD)

            def step(r, masked):
                s = dot(qs[g], kbuf[r, :, lanes], 1, 1) * scale
                if masked:
                    qi = lax.broadcasted_iota(jnp.int32, s.shape, 0) % length + col * length
                    ki = lax.broadcasted_iota(jnp.int32, s.shape, 1)
                    s = jnp.where(ki <= qi, s, LOWEST)
                old = m_sc[...]
                new = jnp.maximum(old, jnp.max(s, axis=1, keepdims=True))
                p = jnp.exp2(s - new)
                f = jnp.exp2(old - new)
                m_sc[...] = new
                l_sc[...] = l_sc[...] * f + jnp.sum(p, axis=1, keepdims=True)
                acc[...] = acc[...] * f + dot(p.astype(BF16), vbuf[r, :, lanes])

            step(row, True)

            @pl.loop(0, row)
            def _(r):
                step(r, False)

            out = (acc[...] / l_sc[...]).astype(BF16)
            for h in range(qper):
                at = pl.multiple_of((g * qper + h) * HD, HD)
                att_out[:, pl.ds(at, HD)] = out[h * length : (h + 1) * length]

    @pl.loop(0, row)
    def _(src):
        for i in range(2):
            relay(i, src).wait_recv()

    for i in range(2):
        own_side(i).wait_recv()
    early = jnp.where(row == rows - 1, kvh, 0)
    attend(0, early)

    dec_copy.wait_recv()

    def p2(j, dst_row):
        return pltpu.make_async_remote_copy(
            src_ref=e_out.at[j], dst_ref=e_in.at[j],
            send_sem=p2_s.at[j], recv_sem=p2_r.at[j],
            device_id={"seq": dst_row * COLS + col}, device_id_type=MESH,
        )

    def p3(j):
        return pltpu.make_async_remote_copy(
            src_ref=p_out.at[j], dst_ref=p_in.at[j],
            send_sem=p3_s.at[j], recv_sem=p3_r.at[j],
            device_id={"seq": partner}, device_id_type=MESH,
        )

    @pl.when(row == 0)
    def _():
        e_in[...] = jnp.zeros(e_in.shape, BF16)

    first_col = col == 0
    for j in range(CHUNKS):
        loc = slice(j * cw, (j + 1) * cw)
        do, dp = dec_own[col, :, loc], dec_par[col, :, loc]
        p1(j).wait_recv()

        @pl.when(row > 0)
        def _():
            p2(j, row).wait_recv()

        so = s_buf[col, j].astype(F32)
        sr = r1[j].astype(F32)
        e = e_in[j].astype(F32)
        earlier = jnp.where(first_col, so, sr)
        later = jnp.where(first_col, sr, so)
        dec_a = jnp.where(first_col, do, dp)
        dec_b = jnp.where(first_col, dp, do)
        mid = dec_a * e + earlier

        @pl.when(row < rows - 1)
        def _():
            e_out[j] = (dec_b * mid + later).astype(BF16)
            p2(j, row + 1).start()

        p_out[j] = jnp.where(first_col, mid, e).astype(BF16)
        p3(j).start()
        ent[j] = jnp.where(first_col, e, mid).astype(BF16)

    attend(early, kvh)

    ones = jnp.ones((8, cw), F32).astype(BF16)
    sums = jnp.zeros((8, length), F32)

    def close(h, j, state):
        loc = slice(j * cw, (j + 1) * cw)
        y = ybuf[h, :, loc] + ex[h, :, loc] * dot(cst[group_of(h, j)], state)
        at = pl.ds(pl.multiple_of(h * half + j * cw, cw), cw)
        y = y * silu(gate_ref[:, at].astype(F32))
        ybuf[h, :, loc] = y
        return y * y

    squares = None
    for j in range(CHUNKS):
        s = close(col, j, ent[j])
        squares = s if squares is None else squares + s
    for j in range(CHUNKS):
        p3(j).wait_recv()
        squares = squares + close(other, j, p_in[j])
    for p in pieces_of(squares, 3):
        sums = sums + dot(ones, p, 1, 1)
    sq_own[...] = sums

    def sq(d):
        return pltpu.make_async_remote_copy(
            src_ref=sq_own, dst_ref=sq_in.at[d - 1],
            send_sem=sq_s.at[d - 1], recv_sem=sq_r.at[d - 1],
            device_id={"tp": (mytp + d) % tp}, device_id_type=MESH,
        )

    for d in range(1, tp):
        sq(d).start()
    for d in range(1, tp):
        sq(d).wait_recv()
        sums = sums + sq_in[d - 1]
    scal = lax.rsqrt(sums / inner + EPS)
    eighth = jnp.full((8, 128), 0.125, F32).astype(BF16)
    column = sum(dot(p, eighth, 0, 0) for p in pieces_of(scal, 3))
    for t in range(width // 128):
        h, loc = (t * 128) // half, (t * 128) % half
        cut = slice(t * 128, (t + 1) * 128)
        mix_out[:, cut] = (ybuf[h, :, loc : loc + 128] * column * gain_ref[:, cut]).astype(BF16)

    for d in range(1, tp):
        sq(d).wait_send()
    for j in range(CHUNKS):
        p1(j).wait_send()
        p3(j).wait_send()
    dec_copy.wait_send()
    for i in range(2):
        own_side(i).wait_send()

    @pl.when(row < rows - 1)
    def _():
        for j in range(CHUNKS):
            p2(j, row + 1).wait_send()

    @pl.when(me < n - 1)
    def _():
        for cp in halo(me + 1):
            cp.wait_send()

    @pl.loop(row + 1, rows)
    def _(dst):
        for i in range(2):
            own_up(i, dst).wait_send()

    @pl.loop(0, row)
    def _(src):
        for i in range(2):
            relay(i, src).wait_send()


def shards(inner, n, tp, x, gate, b, c, step, bias, rate, skip, cx, cb, cc, gain, q, k, v):
    length, width = x.shape
    half = width // 2
    cw = half // CHUNKS
    groups = b.shape[1] // STATE
    kvw = k.shape[1]
    kvh = kvw // HD
    qrows = q.shape[1] // HD // kvh * length
    rows = n // COLS
    vm, dma = pltpu.VMEM, pltpu.SemaphoreType.DMA
    chunk = (CHUNKS, STATE, cw)
    scratch = [
        vm((HALO, width), BF16), vm((HALO, b.shape[1]), BF16), vm((HALO, b.shape[1]), BF16),
        vm((HALO + length, width), F32), vm((2, HALO + length, b.shape[1]), F32),
        vm((2, length, half), F32), vm((2, CHUNKS, length, cw), BF16),
        vm((2, length, half), F32), vm((2, length, half), F32),
        vm((groups, length, STATE), BF16), vm((groups, length, STATE), BF16),
        vm((2,) + chunk, BF16), vm(chunk, BF16), vm(chunk, BF16), vm(chunk, BF16),
        vm(chunk, BF16), vm(chunk, BF16), vm(chunk, BF16),
        vm((2, 1, half), F32), vm((2, 1, half), F32),
        vm((rows, COLS * length, kvw), BF16), vm((rows, COLS * length, kvw), BF16),
        vm((kvh, qrows, HD), BF16), vm((qrows, HD), F32),
        vm((qrows, 1), F32), vm((qrows, 1), F32),
        vm((2, length, half), F32),
        vm((8, length), F32), vm((tp - 1, 8, length), F32),
        dma((3,)), dma((3,)), dma((1,)), dma((1,)),
        dma((CHUNKS,)), dma((CHUNKS,)), dma((CHUNKS,)), dma((CHUNKS,)),
        dma((CHUNKS,)), dma((CHUNKS,)),
        dma((2, rows)), dma((2, rows)), dma((2, rows)), dma((2, rows)), dma((2, 1)),
        dma((tp - 1,)), dma((tp - 1,)),
    ]
    lift = lambda p: p.reshape(1, -1)
    spec = pl.BlockSpec(memory_space=pltpu.VMEM)
    return pl.pallas_call(
        functools.partial(kernel, n, tp, inner),
        out_shape=(
            jax.ShapeDtypeStruct(x.shape, BF16),
            jax.ShapeDtypeStruct(q.shape, BF16),
        ),
        in_specs=[spec] * 15,
        out_specs=(spec, spec),
        scratch_shapes=scratch,
        compiler_params=pltpu.CompilerParams(
            collective_id=0, has_side_effects=True, vmem_limit_bytes=60 * 1024 * 1024
        ),
    )(x, gate, b, c, step, lift(bias), lift(rate), lift(skip), cx, cb, cc, lift(gain), q, k, v)


def solution(mesh):
    n, tp = mesh.shape["seq"], mesh.shape["tp"]
    placed = (
        (P("seq", "tp"),) * 5
        + (P("tp"),) * 3
        + (P(None, "tp"),) * 3
        + (P("tp"),)
        + (P("seq", "tp"),) * 3
    )

    def run(*args):
        inner = args[0].shape[1]
        return jax.shard_map(
            functools.partial(shards, inner, n, tp),
            mesh=mesh,
            in_specs=placed,
            out_specs=(P("seq", "tp"), P("seq", "tp")),
            check_vma=False,
        )(*args)

    return run
```

time: 197 us -> 68.3 us (0.35)
  the two profiles are of different devices: /device:TPU:0 before, /device:TPU:25 now
where the time goes in v1:
time: 68.3 us; the launch traced here: 67.2 us
  Pallas kernels  62.4 us (91%)
  local copies, waits for them, and re-layouts  4.18 us (6%)
    pallas_call x1, Pallas kernels, shards(): pl.pallas_call(functools.partial(kernel, n, tp, inner), out_shape=(jax.Sh...  62.4 us
    unnamed x5, local copies, waits for them, and re-layouts  4.18 us

profile of v1, /device:TPU:25, one launch (start us, length us, event | category | flops | bytes accessed | tf_op | source)
XLA Modules:
  0.0 67.2 jit_solution(471888435910222281)
XLA Ops:
  0.6 1.4 %copy.17.step_ref = f32[128,32]{1,0:T(8,128)} copy(f32[128,32]{0,1:T(8,128)} %param.19) | data formatting | bytes 32768 | tf_op args[4]
  2.1 62.4 %shard_map.158 = (bf16[128,2048]{1,0:T(8,128)(2,1)}, bf16[128,2048]{1,0:T(8,128)(2,1)}) custom-call(bf16[128,2048]{1,0:T(8,128)(2,1)} %x_ref.1, bf16[128,2048]{1,0:T(8,128)(2,1)} %gate_ref.1, bf16[128,256]{1,0:T(8,128)(2,1)} %b_ref.1, bf16[128,256]{1,0:T(8,128)(2,1)} %c_ref.1, f32[128,32]{1,0:T(8,128)} %copy.17.step_ref, f32[1,32]{1,0:T(1,128)} %bitcast.5, ...), custom_call_target="tpu_custom_call" | custom-call | tf_op jit(solution)/shard_map/pallas_call | solution.py:448
  64.5 0.0 copy-start
  64.5 1.9 %copy.20 = bf16[128,2048]{1,0:T(8,128)(2,1)} copy(bf16[128,2048]{1,0:T(8,128)(2,1)} %get-tuple-element.4) | data formatting | bytes 1048576
  66.4 0.0 copy-done
  66.4 0.8 %copy.21 = bf16[128,2048]{1,0:T(8,128)(2,1)} copy(bf16[128,2048]{1,0:T(8,128)(2,1)S(1)} %copy-done) | data formatting | bytes 1048576
Async XLA Ops:
  64.5 2.0 %copy-start = (bf16[128,2048]{1,0:T(8,128)(2,1)S(1)}, bf16[128,2048]{1,0:T(8,128)(2,1)}, u32[]{:S(2)}) copy-start(bf16[128,2048]{1,0:T(8,128)(2,1)} %get-tuple-element.5) | copy-start | bytes 1572868

commit v2 on v1

--- a/solution.py
+++ b/solution.py
@@ -13,8 +13,9 @@
 STATE = 128
 HD = 128
 COLS = 2
-CHUNKS = 4
+CHUNKS = 8
 HALO = 16
+QTILE = 256
 EPS = 1e-05
 LOWEST = -1e30
 MESH = pl.DeviceIdType.MESH
@@ -44,7 +45,7 @@
     x_ref, gate_ref, b_ref, c_ref, step_ref, bias_ref, rate_ref, skip_ref,
     cx_ref, cb_ref, cc_ref, gain_ref, q_ref, k_ref, v_ref,
     mix_out, att_out,
-    hx, hb, hc, padx, padb, sig, wgt, scl, ex, bst, cst,
+    hx, hb, hc, padx, padb, sig, scl, ex, bst, cst,
     s_buf, r1, e_in, e_out, p_out, ent, p_in, dec_own, dec_par,
     kbuf, vbuf, qs, acc, m_sc, l_sc, ybuf, sq_own, sq_in,
     halo_s, halo_r, dec_s, dec_r, p1_s, p1_r, p2_s, p2_r, p3_s, p3_r,
@@ -77,7 +78,11 @@
             barrier, inc=1, device_id={"tp": (mytp + d) % tp}, device_id_type=MESH
         )
 
-    pre = step_ref[...] + bias_ref[...]
+    hr = lax.broadcasted_iota(jnp.int32, (heads, heads), 0)
+    hc_ = lax.broadcasted_iota(jnp.int32, (heads, heads), 1)
+    small = (hr == hc_).astype(F32).astype(BF16)
+    turned = sum(dot(p, small, 0, 0) for p in pieces_of(step_ref[...], 3))
+    pre = turned + bias_ref[...]
     dt = jnp.maximum(pre, 0.0) + jnp.log1p(jnp.exp(-jnp.abs(pre)))
     a = -dt * rate_ref[...]
     ri = lax.broadcasted_iota(jnp.int32, (length, length), 0)
@@ -153,9 +158,6 @@
         for i in range(2):
             own_up(i, dst).start()
 
-    for i in range(2):
-        own_side(i).start()
-
     kbuf[row, place(col)] = k_ref[...]
     vbuf[row, place(col)] = v_ref[...]
     for g in range(kvh):
@@ -193,15 +195,6 @@
         cut = slice(g * STATE, (g + 1) * STATE)
         bst[g] = conv(lambda at: padb[0, at : at + length, cut], cb_ref, cut).astype(BF16)
         cst[g] = conv(lambda at: padb[1, at : at + length, cut], cc_ref, cut).astype(BF16)
-    for h in range(2):
-        for j in range(CHUNKS):
-            cut = slice(h * half + j * cw, h * half + (j + 1) * cw)
-            loc = slice(j * cw, (j + 1) * cw)
-            s = conv(lambda at: padx[at : at + length, cut], cx_ref, cut)
-            wgt[h, j] = (s * sig[h, :, loc]).astype(BF16)
-            sig[h, :, loc] = s
-            scl[h, :, loc] = s * scl[h, :, loc]
-
     def group_of(h, j):
         return h * (groups // 2) + (j * cw) // gwidth
 
@@ -212,11 +205,22 @@
             device_id={"seq": partner}, device_id_type=MESH,
         )
 
-    for j in range(CHUNKS):
-        s_buf[other, j] = dot(bst[group_of(other, j)], wgt[other, j], 0, 0).astype(BF16)
+    def local_state(h, j):
+        loc = slice(j * cw, (j + 1) * cw)
+        cut = pl.ds(pl.multiple_of(h * half + j * cw, 128), cw)
+        u = conv(lambda at: padx[at : at + length, cut], cx_ref, cut)
+        weighted = (u * sig[h, :, loc]).astype(BF16)
+        sig[h, :, loc] = u
+        scl[h, :, loc] = u * scl[h, :, loc]
+        s_buf[h, j] = dot(bst[group_of(h, j)], weighted, 0, 0).astype(BF16)
+
+    for j in range(CHUNKS):
+        local_state(other, j)
         p1(j).start()
-    for j in range(CHUNKS):
-        s_buf[col, j] = dot(bst[group_of(col, j)], wgt[col, j], 0, 0).astype(BF16)
+    for i in range(2):
+        own_side(i).start()
+    for j in range(CHUNKS):
+        local_state(col, j)
 
     @pl.loop(0, row)
     def _(src):
@@ -246,28 +250,33 @@
 
     scale = math.log2(math.e) / math.sqrt(HD)
     qrows = qper * length
+    eye = (ri == ci).astype(F32).astype(BF16)
 
     def attend(lo, hi):
         @pl.loop(lo, hi)
         def _(g):
-            m_sc[...] = jnp.full((qrows, 1), LOWEST, F32)
-            l_sc[...] = jnp.zeros((qrows, 1), F32)
-            acc[...] = jnp.zeros((qrows, HD), F32)
+            m_sc[...] = jnp.full((1, qrows), LOWEST, F32)
+            l_sc[...] = jnp.zeros((1, qrows), F32)
+            acc[...] = jnp.zeros((HD, qrows), F32)
             lanes = pl.ds(pl.multiple_of(g * HD, HD), HD)
 
             def step(r, masked):
-                s = dot(qs[g], kbuf[r, :, lanes], 1, 1) * scale
-                if masked:
-                    qi = lax.broadcasted_iota(jnp.int32, s.shape, 0) % length + col * length
-                    ki = lax.broadcasted_iota(jnp.int32, s.shape, 1)
-                    s = jnp.where(ki <= qi, s, LOWEST)
-                old = m_sc[...]
-                new = jnp.maximum(old, jnp.max(s, axis=1, keepdims=True))
-                p = jnp.exp2(s - new)
-                f = jnp.exp2(old - new)
-                m_sc[...] = new
-                l_sc[...] = l_sc[...] * f + jnp.sum(p, axis=1, keepdims=True)
-                acc[...] = acc[...] * f + dot(p.astype(BF16), vbuf[r, :, lanes])
+                keys = kbuf[r, :, lanes]
+                vals = vbuf[r, :, lanes].T
+                for t in range(qrows // QTILE):
+                    cut = slice(t * QTILE, (t + 1) * QTILE)
+                    s = dot(keys, qs[g, cut], 1, 1) * scale
+                    if masked:
+                        ki = lax.broadcasted_iota(jnp.int32, s.shape, 0)
+                        qi = lax.broadcasted_iota(jnp.int32, s.shape, 1) % length + col * length
+                        s = jnp.where(ki <= qi, s, LOWEST)
+                    old = m_sc[:, cut]
+                    new = jnp.maximum(old, jnp.max(s, axis=0, keepdims=True))
+                    p = jnp.exp2(s - new)
+                    f = jnp.exp2(old - new)
+                    m_sc[:, cut] = new
+                    l_sc[:, cut] = l_sc[:, cut] * f + jnp.sum(p, axis=0, keepdims=True)
+                    acc[:, cut] = acc[:, cut] * f + dot(vals, p.astype(BF16))
 
             step(row, True)
 
@@ -275,10 +284,11 @@
             def _(r):
                 step(r, False)
 
-            out = (acc[...] / l_sc[...]).astype(BF16)
             for h in range(qper):
+                cut = slice(h * length, (h + 1) * length)
+                out = (acc[:, cut] / l_sc[:, cut]).astype(BF16)
                 at = pl.multiple_of((g * qper + h) * HD, HD)
-                att_out[:, pl.ds(at, HD)] = out[h * length : (h + 1) * length]
+                att_out[:, pl.ds(at, HD)] = dot(eye, out, 1, 1).astype(BF16)
 
     @pl.loop(0, row)
     def _(src):
@@ -426,15 +436,15 @@
     scratch = [
         vm((HALO, width), BF16), vm((HALO, b.shape[1]), BF16), vm((HALO, b.shape[1]), BF16),
         vm((HALO + length, width), F32), vm((2, HALO + length, b.shape[1]), F32),
-        vm((2, length, half), F32), vm((2, CHUNKS, length, cw), BF16),
+        vm((2, length, half), F32),
         vm((2, length, half), F32), vm((2, length, half), F32),
         vm((groups, length, STATE), BF16), vm((groups, length, STATE), BF16),
         vm((2,) + chunk, BF16), vm(chunk, BF16), vm(chunk, BF16), vm(chunk, BF16),
         vm(chunk, BF16), vm(chunk, BF16), vm(chunk, BF16),
         vm((2, 1, half), F32), vm((2, 1, half), F32),
         vm((rows, COLS * length, kvw), BF16), vm((rows, COLS * length, kvw), BF16),
-        vm((kvh, qrows, HD), BF16), vm((qrows, HD), F32),
-        vm((qrows, 1), F32), vm((qrows, 1), F32),
+        vm((kvh, qrows, HD), BF16), vm((HD, qrows), F32),
+        vm((1, qrows), F32), vm((1, qrows), F32),
         vm((2, length, half), F32),
         vm((8, length), F32), vm((tp - 1, 8, length), F32),
         dma((3,)), dma((3,)), dma((1,)), dma((1,)),
@@ -457,7 +467,7 @@
         compiler_params=pltpu.CompilerParams(
             collective_id=0, has_side_effects=True, vmem_limit_bytes=60 * 1024 * 1024
         ),
-    )(x, gate, b, c, step, lift(bias), lift(rate), lift(skip), cx, cb, cc, lift(gain), q, k, v)
+    )(x, gate, b, c, step.T, lift(bias), lift(rate), lift(skip), cx, cb, cc, lift(gain), q, k, v)
 
 
 def solution(mesh):

time: 68.3 us -> 50.8 us (0.74); the launches traced: 67.2 us -> 50.7 us
  Pallas kernels: 62.4 us -> 47.3 us
  local copies, waits for them, and re-layouts: 4.18 us -> 2.74 us
    pallas_call x1, Pallas kernels: 62.4 us -> 47.3 us  [shards(): pl.pallas_call(functools.partial(kernel, n, tp, inner), out_shape=(jax.Sh...]
    unnamed x5 -> x4, local copies, waits for them, and re-layouts: 4.18 us -> 2.74 us
where the time goes in v2:
time: 50.8 us; the launch traced here: 50.7 us
  Pallas kernels  47.3 us (93%)
  local copies, waits for them, and re-layouts  2.74 us (5%)
  between operations  0.65 us (1%)
    pallas_call x1, Pallas kernels, shards(): pl.pallas_call(functools.partial(kernel, n, tp, inner), out_shape=(jax.Sh...  47.3 us
    unnamed x4, local copies, waits for them, and re-layouts  2.74 us

profile of v2, /device:TPU:25, one launch (start us, length us, event | category | flops | bytes accessed | tf_op | source)
XLA Modules:
  0.0 50.7 jit_solution(4295907096037941577)
XLA Ops:
  0.6 47.3 %shard_map.158 = (bf16[128,2048]{1,0:T(8,128)(2,1)}, bf16[128,2048]{1,0:T(8,128)(2,1)}) custom-call(bf16[128,2048]{1,0:T(8,128)(2,1)} %x_ref.1, bf16[128,2048]{1,0:T(8,128)(2,1)} %gate_ref.1, bf16[128,256]{1,0:T(8,128)(2,1)} %b_ref.1, bf16[128,256]{1,0:T(8,128)(2,1)} %c_ref.1, f32[32,128]{1,0:T(8,128)} %bitcast.5, f32[1,32]{1,0:T(1,128)} %bitcast.7, ...), custom_call_target="tpu_custom_call" | custom-call | tf_op jit(solution)/shard_map/pallas_call | solution.py:458
  47.9 0.0 copy-start
  47.9 1.9 %copy.19 = bf16[128,2048]{1,0:T(8,128)(2,1)} copy(bf16[128,2048]{1,0:T(8,128)(2,1)} %get-tuple-element.4) | data formatting | bytes 1048576
  49.9 0.0 copy-done
  49.9 0.8 %copy.20 = bf16[128,2048]{1,0:T(8,128)(2,1)} copy(bf16[128,2048]{1,0:T(8,128)(2,1)S(1)} %copy-done) | data formatting | bytes 1048576
Async XLA Ops:
  47.9 2.0 %copy-start = (bf16[128,2048]{1,0:T(8,128)(2,1)S(1)}, bf16[128,2048]{1,0:T(8,128)(2,1)}, u32[]{:S(2)}) copy-start(bf16[128,2048]{1,0:T(8,128)(2,1)} %get-tuple-element.5) | copy-start | bytes 1572868

commit v3 on v2

--- a/solution.py
+++ b/solution.py
@@ -178,6 +178,16 @@
         padx[:HALO] = jnp.zeros((HALO, width), F32)
         padb[:, :HALO] = jnp.zeros((2, HALO, b_ref.shape[1]), F32)
 
+    def pass_on(lo, hi):
+        @pl.loop(lo, hi)
+        def _(at):
+            src = row - 1 - at
+            for i in range(2):
+                kv_copy(i, row, col, src, col, False, kc_s, kc_r, row, src).wait_recv()
+                relay(i, src).start()
+
+    final_row = row == rows - 1
+
     padx[HALO:] = x_ref[...].astype(F32)
     padb[0, HALO:] = b_ref[...].astype(F32)
     padb[1, HALO:] = c_ref[...].astype(F32)
@@ -221,13 +231,6 @@
         own_side(i).start()
     for j in range(CHUNKS):
         local_state(col, j)
-
-    @pl.loop(0, row)
-    def _(src):
-        for i in range(2):
-            own = kv_copy(i, row, col, src, col, False, kc_s, kc_r, row, src)
-            own.wait_recv()
-            relay(i, src).start()
 
     causal = ri >= ci
     lane = lax.broadcasted_iota(jnp.int32, (length, 128), 1)
@@ -248,6 +251,7 @@
                 res = y if res is None else jnp.where(lane >= p * P_SIZE, y, res)
             ybuf[h, :, loc : loc + 128] = res + skipx[:, at : at + 128] * sig[h, :, loc : loc + 128]
 
+    pass_on(0, row)
     scale = math.log2(math.e) / math.sqrt(HD)
     qrows = qper * length
     eye = (ri == ci).astype(F32).astype(BF16)
@@ -290,14 +294,17 @@
                 at = pl.multiple_of((g * qper + h) * HD, HD)
                 att_out[:, pl.ds(at, HD)] = dot(eye, out, 1, 1).astype(BF16)
 
-    @pl.loop(0, row)
-    def _(src):
-        for i in range(2):
-            relay(i, src).wait_recv()
-
+    def gathered(lo, hi):
+        @pl.loop(lo, hi)
+        def _(src):
+            for i in range(2):
+                relay(i, src).wait_recv()
+
+    early = jnp.where(final_row, kvh // 2, 0)
+    soon = jnp.where(final_row, row, 0)
+    gathered(0, soon)
     for i in range(2):
         own_side(i).wait_recv()
-    early = jnp.where(row == rows - 1, kvh, 0)
     attend(0, early)
 
     dec_copy.wait_recv()
@@ -348,6 +355,7 @@
         p3(j).start()
         ent[j] = jnp.where(first_col, e, mid).astype(BF16)
 
+    gathered(soon, row)
     attend(early, kvh)
 
     ones = jnp.ones((8, cw), F32).astype(BF16)

time: 50.8 us -> 46.4 us (0.913)
  Pallas kernels: 47.3 us -> 42.8 us
    pallas_call x1, Pallas kernels: 47.3 us -> 42.8 us  [shards(): pl.pallas_call(functools.partial(kernel, n, tp, inner), out_shape=(jax.Sh...]
where the time goes in v3:
time: 46.4 us; the launch traced here: 46.2 us
  Pallas kernels  42.8 us (92%)
  local copies, waits for them, and re-layouts  2.74 us (6%)
  between operations  0.65 us (1%)
    pallas_call x1, Pallas kernels, shards(): pl.pallas_call(functools.partial(kernel, n, tp, inner), out_shape=(jax.Sh...  42.8 us
    unnamed x4, local copies, waits for them, and re-layouts  2.74 us

profile of v3, /device:TPU:25, one launch (start us, length us, event | category | flops | bytes accessed | tf_op | source)
XLA Modules:
  0.0 46.2 jit_solution(8615736396941322420)
XLA Ops:
  0.6 42.8 %shard_map.158 = (bf16[128,2048]{1,0:T(8,128)(2,1)}, bf16[128,2048]{1,0:T(8,128)(2,1)}) custom-call(bf16[128,2048]{1,0:T(8,128)(2,1)} %x_ref.1, bf16[128,2048]{1,0:T(8,128)(2,1)} %gate_ref.1, bf16[128,256]{1,0:T(8,128)(2,1)} %b_ref.1, bf16[128,256]{1,0:T(8,128)(2,1)} %c_ref.1, f32[32,128]{1,0:T(8,128)} %bitcast.5, f32[1,32]{1,0:T(1,128)} %bitcast.7, ...), custom_call_target="tpu_custom_call" | custom-call | tf_op jit(solution)/shard_map/pallas_call | solution.py:466
  43.5 0.0 copy-start
  43.5 1.9 %copy.19 = bf16[128,2048]{1,0:T(8,128)(2,1)} copy(bf16[128,2048]{1,0:T(8,128)(2,1)} %get-tuple-element.4) | data formatting | bytes 1048576
  45.4 0.0 copy-done
  45.4 0.8 %copy.20 = bf16[128,2048]{1,0:T(8,128)(2,1)} copy(bf16[128,2048]{1,0:T(8,128)(2,1)S(1)} %copy-done) | data formatting | bytes 1048576
Async XLA Ops:
  43.5 2.0 %copy-start = (bf16[128,2048]{1,0:T(8,128)(2,1)S(1)}, bf16[128,2048]{1,0:T(8,128)(2,1)}, u32[]{:S(2)}) copy-start(bf16[128,2048]{1,0:T(8,128)(2,1)} %get-tuple-element.5) | copy-start | bytes 1572868
